TPU v7x, 32 devices: a whole 2x2x4 slice. The times are simulated.
32 devices in a mesh: dp: 4 (over x, core), ep: 8 (over z, y).
Axes of the slice: x: 2, y: 2, z: 4, core: 2. Of those that a mesh axis runs over, the one named last changes fastest.
Arguments:
- tokens: bfloat16 [4096, 2048], P(('dp', 'ep')), parts along dimension 0, may hold values from -6 to 6
- expert_ids: int32 [4096, 8], P(('dp', 'ep')), parts along dimension 0, may hold values from 0 to 15, all different within a row; in each aligned block of 32 rows (0 to 31, 32 to 63, ...) at most 32 rows name the same one
- gate_nums: int32 [4096, 8], P(('dp', 'ep')), parts along dimension 0, may hold values from 64 to 1023
- w_gate: bfloat16 [16, 2048, 768], P('ep'), may hold values from -0.125 to 0.125
- w_up: bfloat16 [16, 2048, 768], P('ep'), may hold values from -0.125 to 0.125
- w_down: bfloat16 [16, 768, 2048], P('ep'), may hold values from -0.21875 to 0.21875
Outputs:
- mixed: bfloat16 [4096, 2048], P(('dp', 'ep')), parts along dimension 0
There are 4 independent parts, one for each index of `dp`. A program takes and returns all parts, laid end to end along the dimension named above; an argument that names none is the same for every part. Nothing has to cross between parts.
Inputs may be any that keep to these rules, and one draw needn't show every extreme that they name: `expert_ids`: each row names 8 different experts. In every aligned block of 32 rows no expert is named by more than 32 rows, a bound that some block reaches.
All inputs are finite; a program needn't handle non-finite values.
Results may differ from a plain program's by a relative error of at most 0.008.
Values may be sent and summed in bfloat16 or wider, within the bound.
A program may use at most 128 MiB of HBM per device.

v0:
```python
import jax
import jax.numpy as jnp
from jax import lax
from jax.sharding import PartitionSpec as P

TOP = 8
BLOCKS = 4


denominator = 1024.0


def shards(tokens, expert_ids, gate_nums, w_gate, w_up, w_down):
    ways = lax.axis_size("ep")
    local = w_gate.shape[0]
    experts = local * ways
    width = tokens.shape[1]
    block_rows = tokens.shape[0] // BLOCKS
    slots = 2 * block_rows * TOP // experts
    gates = gate_nums.astype(jnp.float32) / denominator
    labels = jnp.arange(experts, dtype=jnp.int32)
    slot_ids = jnp.arange(slots, dtype=jnp.int32)

    def expert_work(received):
        gate = jnp.einsum("sxcd,xdf->sxcf", received, w_gate, preferred_element_type=jnp.float32)
        up = jnp.einsum("sxcd,xdf->sxcf", received, w_up, preferred_element_type=jnp.float32)
        hidden = (jax.nn.silu(gate) * up).astype(jnp.bfloat16)
        result = jnp.einsum("sxcf,xfd->sxcd", hidden, w_down, preferred_element_type=jnp.float32)
        return lax.all_to_all(
            result.astype(jnp.bfloat16), "ep", split_axis=0, concat_axis=0, tiled=True
        )

    places = []
    weights = []
    buffers = []
    for block in range(BLOCKS):
        lower = block * block_rows
        ids_blk = expert_ids[lower : lower + block_rows]
        gates_blk = gates[lower : lower + block_rows]
        rows_blk = tokens[lower : lower + block_rows]
        onehot = ids_blk[:, :, None] == labels[None, None, :]
        member = jnp.sum(onehot.astype(jnp.int32), axis=1)
        before = jnp.cumsum(member, axis=0) - member
        place = (before[:, :, None] == slot_ids[None, None, :]) & (member[:, :, None] > 0)
        weight = jnp.sum(jnp.where(onehot, gates_blk[:, :, None], 0.0), axis=1)
        packed = jnp.einsum(
            "bec,bd->ecd", place.astype(jnp.bfloat16), rows_blk, preferred_element_type=jnp.float32
        )
        buffers.append(packed.astype(jnp.bfloat16).reshape(ways, local, slots, width))
        places.append(place)
        weights.append(weight)
    backs = [
        expert_work(lax.all_to_all(buffers[block], "ep", split_axis=0, concat_axis=0, tiled=True))
        for block in range(BLOCKS)
    ]
    outputs = []
    for block in range(BLOCKS):
        back = backs[block].reshape(experts, slots, width)
        mixing = jnp.where(places[block], weights[block][:, :, None], 0.0)
        high = mixing.astype(jnp.bfloat16)
        low = (mixing - high.astype(jnp.float32)).astype(jnp.bfloat16)
        part_high = jnp.einsum("bec,ecd->bd", high, back, preferred_element_type=jnp.float32)
        part_low = jnp.einsum("bec,ecd->bd", low, back, preferred_element_type=jnp.float32)
        outputs.append(part_high + part_low)
    return jnp.concatenate(outputs, axis=0).astype(jnp.bfloat16)


def solution(mesh):
    placed = (
        P(("dp", "ep"), None),
        P(("dp", "ep"), None),
        P(("dp", "ep"), None),
        P("ep", None, None),
        P("ep", None, None),
        P("ep", None, None),
    )
    return jax.shard_map(
        shards, mesh=mesh, in_specs=placed, out_specs=P(("dp", "ep"), None), check_vma=False
    )
```

profile of v0, /device:TPU:0, one launch (start us, length us, event | category | flops | bytes accessed | tf_op | source)
XLA Modules:
  0.0 430.7 jit_solution(11209908846326911032)
XLA Ops:
  0.0 0.9 fusion.193
  0.9 0.1 copy.91
  1.2 3.3 convolution_convert_fusion.3
  4.4 7.4 %all-to-all-start = ((bf16[8,2,32,2048]{3,2,1,0:T(8,128)(2,1)}), bf16[8,2,32,2048]{3,2,1,0:T(8,128)(2,1)S(1)}, u32[]{:S(2)}, u32[]{:S(2)}) async-start(bf16[8,2,32,2048]{3,2,1,0:T(8,128)(2,1)} %bitcast.1), calls=%async_computation | async-start | bytes 4194304 | tf_op jit(solution)/shard_map/all_to_all | solution.py:53
  11.9 0.1 copy.98
  12.0 0.1 copy.100
  12.1 2.3 convolution_convert_fusion.2
  14.4 45.7 %all-to-all-done = bf16[8,2,32,2048]{3,2,1,0:T(8,128)(2,1)S(1)} async-done(((bf16[8,2,32,2048]{3,2,1,0:T(8,128)(2,1)}), bf16[8,2,32,2048]{3,2,1,0:T(8,128)(2,1)S(1)}, u32[]{:S(2)}, u32[]{:S(2)}) %all-to-all-start) | async-done | bytes 2097184 | tf_op jit(solution)/shard_map/all_to_all | solution.py:53
  60.1 4.3 %all-to-all-start.2 = ((bf16[8,2,32,2048]{3,2,1,0:T(8,128)(2,1)}), bf16[8,2,32,2048]{3,2,1,0:T(8,128)(2,1)}, u32[]{:S(2)}, u32[]{:S(2)}) async-start(bf16[8,2,32,2048]{3,2,1,0:T(8,128)(2,1)} %bitcast.15), calls=%async_computation.2 | async-start | bytes 4194304 | tf_op jit(solution)/shard_map/all_to_all | solution.py:53
  64.5 0.1 copy.105
  64.7 2.4 convolution_convert_fusion.1
  67.1 45.2 %all-to-all-done.2 = bf16[8,2,32,2048]{3,2,1,0:T(8,128)(2,1)} async-done(((bf16[8,2,32,2048]{3,2,1,0:T(8,128)(2,1)}), bf16[8,2,32,2048]{3,2,1,0:T(8,128)(2,1)}, u32[]{:S(2)}, u32[]{:S(2)}) %all-to-all-start.2) | async-done | bytes 2097184 | tf_op jit(solution)/shard_map/all_to_all | solution.py:53
  112.3 4.4 %all-to-all-start.4 = ((bf16[8,2,32,2048]{3,2,1,0:T(8,128)(2,1)}), bf16[8,2,32,2048]{3,2,1,0:T(8,128)(2,1)}, u32[]{:S(2)}, u32[]{:S(2)}) async-start(bf16[8,2,32,2048]{3,2,1,0:T(8,128)(2,1)} %bitcast.26), calls=%async_computation.4 | async-start | bytes 4194304 | tf_op jit(solution)/shard_map/all_to_all | solution.py:53
  116.7 0.1 copy.112
  116.9 2.4 convolution_convert_fusion
  119.3 45.1 %all-to-all-done.4 = bf16[8,2,32,2048]{3,2,1,0:T(8,128)(2,1)} async-done(((bf16[8,2,32,2048]{3,2,1,0:T(8,128)(2,1)}), bf16[8,2,32,2048]{3,2,1,0:T(8,128)(2,1)}, u32[]{:S(2)}, u32[]{:S(2)}) %all-to-all-start.4) | async-done | bytes 2097184 | tf_op jit(solution)/shard_map/all_to_all | solution.py:53
  164.5 4.3 %all-to-all-start.6 = ((bf16[8,2,32,2048]{3,2,1,0:T(8,128)(2,1)}), bf16[8,2,32,2048]{3,2,1,0:T(8,128)(2,1)}, u32[]{:S(2)}, u32[]{:S(2)}) async-start(bf16[8,2,32,2048]{3,2,1,0:T(8,128)(2,1)} %bitcast.34), calls=%async_computation.6 | async-start | bytes 4194304 | tf_op jit(solution)/shard_map/all_to_all | solution.py:53
  168.8 5.7 %fusion.22 = f32[2,8,32,768]{3,2,1,0:T(8,128)} fusion(bf16[2,2048,768]{2,1,0:T(8,128)(2,1)} %param.9, bf16[8,2,32,2048]{3,2,1,0:T(8,128)(2,1)S(1)} %all-to-all-done), kind=kOutput, calls=%fused_computation.22 | convolution fusion | flops 1610612736 | bytes 9961472 | tf_op jit(solution)/shard_map/sxcd,xdf->sxcf/dot_general | solution.py:25
  174.5 9.9 %fusion.45 = bf16[8,2,32,2048]{3,2,0,1:T(8,128)(2,1)} fusion(bf16[2,768,2048]{2,1,0:T(8,128)(2,1)} %param.11, f32[2,8,32,768]{3,2,1,0:T(8,128)} %fusion.22, bf16[2,2048,768]{2,1,0:T(8,128)(2,1)} %param.10, bf16[8,2,32,2048]{3,2,1,0:T(8,128)(2,1)S(1)} %all-to-all-done), kind=kOutput, calls=%fused_computation.35 | convolution fusion | flops 3224633344 | bytes 18350080 | tf_op jit(solution)/shard_map/sxcf,xfd->sxcd/dot_general | solution.py:28
  184.4 3.2 copy.97
  187.6 29.0 %all-to-all-done.6 = bf16[8,2,32,2048]{3,2,1,0:T(8,128)(2,1)} async-done(((bf16[8,2,32,2048]{3,2,1,0:T(8,128)(2,1)}), bf16[8,2,32,2048]{3,2,1,0:T(8,128)(2,1)}, u32[]{:S(2)}, u32[]{:S(2)}) %all-to-all-start.6) | async-done | bytes 2097184 | tf_op jit(solution)/shard_map/all_to_all | solution.py:53
  216.6 3.8 all-to-all-start.1
  220.4 6.4 %fusion.20 = f32[2,8,32,768]{3,2,1,0:T(8,128)} fusion(bf16[2,2048,768]{2,1,0:T(8,128)(2,1)} %param.9, bf16[8,2,32,2048]{3,2,1,0:T(8,128)(2,1)} %all-to-all-done.2), kind=kOutput, calls=%fused_computation.20 | convolution fusion | flops 1610612736 | bytes 9961472 | tf_op jit(solution)/shard_map/sxcd,xdf->sxcf/dot_general | solution.py:25
  226.9 10.5 %fusion.42 = bf16[8,2,32,2048]{3,2,0,1:T(8,128)(2,1)} fusion(bf16[2,768,2048]{2,1,0:T(8,128)(2,1)} %param.11, f32[2,8,32,768]{3,2,1,0:T(8,128)} %fusion.20, bf16[2,2048,768]{2,1,0:T(8,128)(2,1)} %param.10, bf16[8,2,32,2048]{3,2,1,0:T(8,128)(2,1)} %all-to-all-done.2), kind=kOutput, calls=%fused_computation.34 | convolution fusion | flops 3224633344 | bytes 18350080 | tf_op jit(solution)/shard_map/sxcf,xfd->sxcd/dot_general | solution.py:28
  237.3 3.2 copy.104
  240.6 28.2 %all-to-all-done.1 = bf16[8,2,32,2048]{3,2,1,0:T(8,128)(2,1)S(1)} async-done(((bf16[8,2,32,2048]{3,2,1,0:T(8,128)(2,1)}), bf16[8,2,32,2048]{3,2,1,0:T(8,128)(2,1)S(1)}, u32[]{:S(2)}, u32[]{:S(2)}) %all-to-all-start.1) | async-done | bytes 2097184 | tf_op jit(solution)/shard_map/all_to_all | solution.py:29
  268.7 4.3 %all-to-all-start.3 = ((bf16[8,2,32,2048]{3,2,1,0:T(8,128)(2,1)}), bf16[8,2,32,2048]{3,2,1,0:T(8,128)(2,1)}, u32[]{:S(2)}, u32[]{:S(2)}) async-start(bf16[8,2,32,2048]{3,2,1,0:T(8,128)(2,1)} %copy.104), calls=%async_computation.3 | async-start | bytes 4194304 | tf_op jit(solution)/shard_map/all_to_all | solution.py:29
  273.1 6.4 %fusion.18 = f32[2,8,32,768]{3,2,1,0:T(8,128)} fusion(bf16[2,2048,768]{2,1,0:T(8,128)(2,1)} %param.9, bf16[8,2,32,2048]{3,2,1,0:T(8,128)(2,1)} %all-to-all-done.4), kind=kOutput, calls=%fused_computation.18 | convolution fusion | flops 1610612736 | bytes 9961472 | tf_op jit(solution)/shard_map/sxcd,xdf->sxcf/dot_general | solution.py:25
  279.4 10.5 %fusion.39 = bf16[8,2,32,2048]{3,2,0,1:T(8,128)(2,1)} fusion(bf16[2,768,2048]{2,1,0:T(8,128)(2,1)} %param.11, f32[2,8,32,768]{3,2,1,0:T(8,128)} %fusion.18, bf16[2,2048,768]{2,1,0:T(8,128)(2,1)} %param.10, bf16[8,2,32,2048]{3,2,1,0:T(8,128)(2,1)} %all-to-all-done.4), kind=kOutput, calls=%fused_computation.33 | convolution fusion | flops 3224633344 | bytes 18350080 | tf_op jit(solution)/shard_map/sxcf,xfd->sxcd/dot_general | solution.py:28
  289.9 3.2 copy.111
  293.1 27.8 %all-to-all-done.3 = bf16[8,2,32,2048]{3,2,1,0:T(8,128)(2,1)} async-done(((bf16[8,2,32,2048]{3,2,1,0:T(8,128)(2,1)}), bf16[8,2,32,2048]{3,2,1,0:T(8,128)(2,1)}, u32[]{:S(2)}, u32[]{:S(2)}) %all-to-all-start.3) | async-done | bytes 2097184 | tf_op jit(solution)/shard_map/all_to_all | solution.py:29
  320.9 4.6 %all-to-all-start.5 = ((bf16[8,2,32,2048]{3,2,1,0:T(8,128)(2,1)}), bf16[8,2,32,2048]{3,2,1,0:T(8,128)(2,1)}, u32[]{:S(2)}, u32[]{:S(2)}) async-start(bf16[8,2,32,2048]{3,2,1,0:T(8,128)(2,1)} %copy.111), calls=%async_computation.5 | async-start | bytes 4194304 | tf_op jit(solution)/shard_map/all_to_all | solution.py:29
  325.5 6.4 %fusion.16 = f32[2,8,32,768]{3,2,1,0:T(8,128)} fusion(bf16[2,2048,768]{2,1,0:T(8,128)(2,1)} %param.9, bf16[8,2,32,2048]{3,2,1,0:T(8,128)(2,1)} %all-to-all-done.6), kind=kOutput, calls=%fused_computation.16 | convolution fusion | flops 1610612736 | bytes 9961472 | tf_op jit(solution)/shard_map/sxcd,xdf->sxcf/dot_general | solution.py:25
  331.8 10.6 %fusion.36 = bf16[8,2,32,2048]{3,2,0,1:T(8,128)(2,1)} fusion(bf16[2,768,2048]{2,1,0:T(8,128)(2,1)} %param.11, f32[2,8,32,768]{3,2,1,0:T(8,128)} %fusion.16, bf16[2,2048,768]{2,1,0:T(8,128)(2,1)} %param.10, bf16[8,2,32,2048]{3,2,1,0:T(8,128)(2,1)} %all-to-all-done.6), kind=kOutput, calls=%fused_computation.32 | convolution fusion | flops 3224633344 | bytes 18350080 | tf_op jit(solution)/shard_map/sxcf,xfd->sxcd/dot_general | solution.py:28
  342.4 3.2 copy.118
  345.6 27.6 %all-to-all-done.5 = bf16[8,2,32,2048]{3,2,1,0:T(8,128)(2,1)} async-done(((bf16[8,2,32,2048]{3,2,1,0:T(8,128)(2,1)}), bf16[8,2,32,2048]{3,2,1,0:T(8,128)(2,1)}, u32[]{:S(2)}, u32[]{:S(2)}) %all-to-all-start.5) | async-done | bytes 2097184 | tf_op jit(solution)/shard_map/all_to_all | solution.py:29
  373.1 4.4 %all-to-all-start.7 = ((bf16[8,2,32,2048]{3,2,1,0:T(8,128)(2,1)}), bf16[8,2,32,2048]{3,2,1,0:T(8,128)(2,1)}, u32[]{:S(2)}, u32[]{:S(2)}) async-start(bf16[8,2,32,2048]{3,2,1,0:T(8,128)(2,1)} %copy.118), calls=%async_computation.7 | async-start | bytes 4194304 | tf_op jit(solution)/shard_map/all_to_all | solution.py:29
  377.5 0.1 fusion.192
  377.6 0.8 convolution_bitcast_fusion.6
  378.4 2.3 convolution_bitcast_fusion.4
  380.7 2.3 convolution_bitcast_fusion.2
  383.1 0.8 fusion.55
  383.9 2.4 fusion.54
  386.2 2.3 fusion.53
  388.6 36.6 %all-to-all-done.7 = bf16[8,2,32,2048]{3,2,1,0:T(8,128)(2,1)} async-done(((bf16[8,2,32,2048]{3,2,1,0:T(8,128)(2,1)}), bf16[8,2,32,2048]{3,2,1,0:T(8,128)(2,1)}, u32[]{:S(2)}, u32[]{:S(2)}) %all-to-all-start.7) | async-done | bytes 2097184 | tf_op jit(solution)/shard_map/all_to_all | solution.py:29
  425.2 2.3 convolution_bitcast_fusion
  427.5 2.3 fusion.52
  429.9 0.8 pad_maximum_fusion
  (24 shorter events, 0.6 us)
Async XLA Ops:
  4.4 7.7 %copy-start = (bf16[128,2048]{1,0:T(8,128)(2,1)S(1)}, bf16[128,2048]{1,0:T(8,128)(2,1)}, u32[]{:S(2)}) copy-start(bf16[128,2048]{1,0:T(8,128)(2,1)} %param.6) | copy-start | bytes 1572868
  4.4 55.7 %all-to-all-start = ((bf16[8,2,32,2048]{3,2,1,0:T(8,128)(2,1)}), bf16[8,2,32,2048]{3,2,1,0:T(8,128)(2,1)S(1)}, u32[]{:S(2)}, u32[]{:S(2)}) async-start(bf16[8,2,32,2048]{3,2,1,0:T(8,128)(2,1)} %bitcast.1), calls=%async_computation | async-start | bytes 4194304 | tf_op jit(solution)/shard_map/all_to_all | solution.py:53
  60.1 52.2 %all-to-all-start.2 = ((bf16[8,2,32,2048]{3,2,1,0:T(8,128)(2,1)}), bf16[8,2,32,2048]{3,2,1,0:T(8,128)(2,1)}, u32[]{:S(2)}, u32[]{:S(2)}) async-start(bf16[8,2,32,2048]{3,2,1,0:T(8,128)(2,1)} %bitcast.15), calls=%async_computation.2 | async-start | bytes 4194304 | tf_op jit(solution)/shard_map/all_to_all | solution.py:53
  112.3 52.2 %all-to-all-start.4 = ((bf16[8,2,32,2048]{3,2,1,0:T(8,128)(2,1)}), bf16[8,2,32,2048]{3,2,1,0:T(8,128)(2,1)}, u32[]{:S(2)}, u32[]{:S(2)}) async-start(bf16[8,2,32,2048]{3,2,1,0:T(8,128)(2,1)} %bitcast.26), calls=%async_computation.4 | async-start | bytes 4194304 | tf_op jit(solution)/shard_map/all_to_all | solution.py:53
  164.5 52.2 %all-to-all-start.6 = ((bf16[8,2,32,2048]{3,2,1,0:T(8,128)(2,1)}), bf16[8,2,32,2048]{3,2,1,0:T(8,128)(2,1)}, u32[]{:S(2)}, u32[]{:S(2)}) async-start(bf16[8,2,32,2048]{3,2,1,0:T(8,128)(2,1)} %bitcast.34), calls=%async_computation.6 | async-start | bytes 4194304 | tf_op jit(solution)/shard_map/all_to_all | solution.py:53
  216.6 52.1 %all-to-all-start.1 = ((bf16[8,2,32,2048]{3,2,1,0:T(8,128)(2,1)}), bf16[8,2,32,2048]{3,2,1,0:T(8,128)(2,1)S(1)}, u32[]{:S(2)}, u32[]{:S(2)}) async-start(bf16[8,2,32,2048]{3,2,1,0:T(8,128)(2,1)} %copy.97), calls=%async_computation.1 | async-start | bytes 4194304 | tf_op jit(solution)/shard_map/all_to_all | solution.py:29
  268.7 52.1 %all-to-all-start.3 = ((bf16[8,2,32,2048]{3,2,1,0:T(8,128)(2,1)}), bf16[8,2,32,2048]{3,2,1,0:T(8,128)(2,1)}, u32[]{:S(2)}, u32[]{:S(2)}) async-start(bf16[8,2,32,2048]{3,2,1,0:T(8,128)(2,1)} %copy.104), calls=%async_computation.3 | async-start | bytes 4194304 | tf_op jit(solution)/shard_map/all_to_all | solution.py:29
  320.9 52.3 %all-to-all-start.5 = ((bf16[8,2,32,2048]{3,2,1,0:T(8,128)(2,1)}), bf16[8,2,32,2048]{3,2,1,0:T(8,128)(2,1)}, u32[]{:S(2)}, u32[]{:S(2)}) async-start(bf16[8,2,32,2048]{3,2,1,0:T(8,128)(2,1)} %copy.111), calls=%async_computation.5 | async-start | bytes 4194304 | tf_op jit(solution)/shard_map/all_to_all | solution.py:29
  345.6 31.9 %copy-start.1 = (s32[128,8]{0,1:T(8,128)S(1)}, s32[128,8]{0,1:T(8,128)}, u32[]{:S(2)}) copy-start(s32[128,8]{0,1:T(8,128)} %param.8) | copy-start | bytes 12292
  373.1 52.1 %all-to-all-start.7 = ((bf16[8,2,32,2048]{3,2,1,0:T(8,128)(2,1)}), bf16[8,2,32,2048]{3,2,1,0:T(8,128)(2,1)}, u32[]{:S(2)}, u32[]{:S(2)}) async-start(bf16[8,2,32,2048]{3,2,1,0:T(8,128)(2,1)} %copy.118), calls=%async_computation.7 | async-start | bytes 4194304 | tf_op jit(solution)/shard_map/all_to_all | solution.py:29
where the time goes:
time: 432 us; the launch traced here: 431 us
  waiting for transfers between devices  285 us (66%)
  matrix products  92.3 us (21%)
  starting transfers between devices  37.5 us (9%)
  local copies, waits for them, and re-layouts  14.4 us (3%)
    all_to_all x4, waiting for transfers between devices, shards(): lax.all_to_all(buffers[block], 'ep', split_axis=0, concat_axis=0, tiled=T...  165 us
    all_to_all x4, waiting for transfers between devices, expert_work(): lax.all_to_all(result.astype(jnp.bfloat16), 'ep', split_axis=0, concat_ax...  120 us
    dot_general x4, matrix products, expert_work(): jnp.einsum('sxcf,xfd->sxcd', hidden, w_down, preferred_element_type=jnp.f...  41.4 us
    dot_general x4, matrix products, expert_work(): jnp.einsum('sxcd,xdf->sxcf', received, w_gate, preferred_element_type=jnp...  24.9 us
    all_to_all x4, starting transfers between devices, shards(): lax.all_to_all(buffers[block], 'ep', split_axis=0, concat_axis=0, tiled=T...  20.5 us
    all_to_all x4, starting transfers between devices, expert_work(): lax.all_to_all(result.astype(jnp.bfloat16), 'ep', split_axis=0, concat_ax...  17.1 us
    convert_element_type x4, local copies, waits for them, and re-layouts, expert_work(): result.astype(jnp.bfloat16)  12.8 us
    dot_general x4, matrix products, shards(): jnp.einsum('bec,bd->ecd', place.astype(jnp.bfloat16), rows_blk, preferred...  10.5 us
  transfers between devices with their start and end apart: 8, of which 8 were waited for; matrix products, arithmetic and copies ran while one was open for 23% of the time, Pallas kernels for 0%

commit v1 on v0

v1 whole, which is shorter than its diff:
```python
import jax
import jax.numpy as jnp
from jax import lax
from jax.sharding import PartitionSpec as P

denominator = 1024.0


def shards(tokens, expert_ids, gate_nums, w_gate, w_up, w_down):
    ways = lax.axis_size("ep")
    local = w_gate.shape[0]
    experts = local * ways
    gates = gate_nums.astype(jnp.float32) / denominator
    labels = jnp.arange(experts, dtype=jnp.int32)
    onehot = expert_ids[:, :, None] == labels[None, None, :]
    weight = jnp.sum(jnp.where(onehot, gates[:, :, None], 0.0), axis=1)
    weights = lax.all_to_all(weight, "ep", split_axis=1, concat_axis=0, tiled=True)
    rows = lax.all_gather(tokens, "ep", axis=0, tiled=True)
    gate = jnp.einsum("td,xdf->xtf", rows, w_gate, preferred_element_type=jnp.float32)
    up = jnp.einsum("td,xdf->xtf", rows, w_up, preferred_element_type=jnp.float32)
    hidden = (jax.nn.silu(gate) * up * weights.T[:, :, None]).astype(jnp.bfloat16)
    result = jnp.einsum("xtf,xfd->td", hidden, w_down, preferred_element_type=jnp.float32)
    return lax.psum_scatter(
        result.astype(jnp.bfloat16), "ep", scatter_dimension=0, tiled=True
    )


def solution(mesh):
    placed = (
        P(("dp", "ep"), None),
        P(("dp", "ep"), None),
        P(("dp", "ep"), None),
        P("ep", None, None),
        P("ep", None, None),
        P("ep", None, None),
    )
    return jax.shard_map(
        shards, mesh=mesh, in_specs=placed, out_specs=P(("dp", "ep"), None), check_vma=False
    )
```

time: 432 us -> 214 us (0.50)
  waiting for transfers between devices: 285 us -> 156 us
  matrix products: 92.3 us -> 34.5 us
  starting transfers between devices: 37.5 us -> 7.35 us
  local copies, waits for them, and re-layouts: 14.4 us -> 0 us
  between operations: 0.16 us -> 13.4 us
    all_to_all x8 -> x1, waiting for transfers between devices: 285 us -> 0.01 us  [shards(): lax.all_to_all(weight, 'ep', split_axis=1, concat_axis=0, tiled=True)]
    reduce_scatter x0 -> x1, waiting for transfers between devices: none -> 87.4 us  [shards(): lax.psum_scatter(result.astype(jnp.bfloat16), 'ep', scatter_dimension=0,...]
    all_gather x0 -> x1, waiting for transfers between devices: none -> 68.4 us  [shards(): rows = lax.all_gather(tokens, 'ep', axis=0, tiled=True)]
    dot_general x20 -> x2, matrix products: 92.3 us -> 34.5 us  [the longest x1 22.8 us: shards(): jnp.einsum('xtf,xfd->td', hidden, w_down, preferred_element_type=jnp.floa...]
    all_to_all x8 -> x1, starting transfers between devices: 37.5 us -> 7.31 us  [shards(): lax.all_to_all(weight, 'ep', split_axis=1, concat_axis=0, tiled=True)]
    convert_element_type x4 -> x0, local copies, waits for them, and re-layouts: 12.8 us -> none  [expert_work(): result.astype(jnp.bfloat16)]
  transfers between devices with their start and end apart: 8 -> 3, of which waited for: 8 -> 2; matrix products, arithmetic and copies ran while one was open for 23% -> 6% of each run, Pallas kernels for 0% -> 0%
where the time goes in v1:
time: 214 us
  waiting for transfers between devices  156 us (73%)
  matrix products  34.5 us (16%)
  between operations  13.4 us (6%)
  starting transfers between devices  7.35 us (3%)
    reduce_scatter x1, waiting for transfers between devices, shards(): lax.psum_scatter(result.astype(jnp.bfloat16), 'ep', scatter_dimension=0,...  87.4 us
    all_gather x1, waiting for transfers between devices, shards(): rows = lax.all_gather(tokens, 'ep', axis=0, tiled=True)  68.4 us
    dot_general x1, matrix products, shards(): jnp.einsum('xtf,xfd->td', hidden, w_down, preferred_element_type=jnp.floa...  22.8 us
    dot_general x1, matrix products, shards(): jnp.einsum('td,xdf->xtf', rows, w_up, preferred_element_type=jnp.float32)  11.8 us
    all_to_all x1, starting transfers between devices, shards(): lax.all_to_all(weight, 'ep', split_axis=1, concat_axis=0, tiled=True)  7.31 us
  transfers between devices with their start and end apart: 3, of which 2 were waited for; matrix products, arithmetic and copies ran while one was open for 6% of the time, Pallas kernels for 0%

profile of v1, /device:TPU:0, one launch (start us, length us, event | category | flops | bytes accessed | tf_op | source)
XLA Modules:
  0.0 213.8 jit_solution(13335941357443734018)
XLA Ops:
  6.5 0.0 all-gather.2.cloned.1.call-start
  6.5 0.7 all-gather.2.cloned.1.call-update
  7.3 0.7 convert_multiply_fusion
  7.9 1.3 select_reduce_fusion
  9.2 7.3 %all-to-all-start = ((f32[128,8,2]{0,2,1:T(2,128)}), f32[128,8,2]{0,2,1:T(2,128)S(1)}, u32[]{:S(2)}, u32[]{:S(2)}) async-start(f32[128,8,2]{0,2,1:T(2,128)} %bitcast.3), calls=%async_computation | async-start | bytes 16384 | tf_op jit(solution)/shard_map/all_to_all | solution.py:17
  16.6 0.0 reduce-scatter.2.cloned.1.call-start
  16.6 68.4 %all-gather.2.cloned.1.call-done = bf16[1024,2048]{1,0:T(8,128)(2,1)} async-done(((bf16[128,2048]{1,0:T(8,128)(2,1)}), bf16[1024,2048]{1,0:T(8,128)(2,1)}) %all-gather.2.cloned.1.call-update) | async-done | bytes 4194320 | tf_op jit(solution)/shard_map/all_gather | solution.py:18
  85.0 11.8 %fusion.5 = f32[2,768,1024]{2,1,0:T(8,128)} fusion(bf16[2,2048,768]{2,1,0:T(8,128)(2,1)} %param.10, bf16[1024,2048]{1,0:T(8,128)(2,1)} %all-gather.2.cloned.1.call-done), kind=kOutput, calls=%fused_computation.9 | convolution fusion | flops 6442450944 | bytes 16777216 | tf_op jit(solution)/shard_map/td,xdf->xtf/dot_general | solution.py:20
  96.8 0.0 all-to-all-done
  96.8 22.8 %bitcast_convert_fusion = bf16[1024,2048]{1,0:T(8,128)(2,1)} fusion(bf16[2,768,2048]{2,1,0:T(8,128)(2,1)} %param.11, f32[2,768,1024]{2,1,0:T(8,128)} %fusion.5, bf16[2,2048,768]{2,1,0:T(8,128)(2,1)} %param.9, bf16[1024,2048]{1,0:T(8,128)(2,1)} %all-gather.2.cloned.1.call-done, f32[2,1024]{1,0:T(2,128)S(1)} %bitcast.54), kind=kOutput, calls=%fused_computation | convolution fusion | flops 12898009088 | bytes 27271168 | tf_op jit(solution)/shard_map/xtf,xfd->td/dot_general | solution.py:22
  119.5 0.0 reduce-scatter.2.cloned.1.call-update
  119.6 87.4 %reduce-scatter.2.cloned.1.call-done = bf16[128,2048]{1,0:T(8,128)(2,1)} async-done(((bf16[1024,2048]{1,0:T(8,128)(2,1)}), bf16[128,2048]{1,0:T(8,128)(2,1)}) %reduce-scatter.2.cloned.1.call-update) | async-done | bytes 524304 | tf_op jit(solution)/shard_map/reduce_scatter | solution.py:23
Async XLA Ops:
  6.5 78.5 %all-gather.2.cloned.1.call-start = ((), (), s32[]{:S(2)}) async-start(), calls=%async_computation.2 | async-start | bytes 4718592 | tf_op jit(solution)/shard_map/all_gather | solution.py:18
  9.2 87.5 %all-to-all-start = ((f32[128,8,2]{0,2,1:T(2,128)}), f32[128,8,2]{0,2,1:T(2,128)S(1)}, u32[]{:S(2)}, u32[]{:S(2)}) async-start(f32[128,8,2]{0,2,1:T(2,128)} %bitcast.3), calls=%async_computation | async-start | bytes 16384 | tf_op jit(solution)/shard_map/all_to_all | solution.py:17
  16.6 190.4 %reduce-scatter.2.cloned.1.call-start = ((), (), s32[]{:S(2)}) async-start(), calls=%async_computation.3 | async-start | bytes 4718592 | tf_op jit(solution)/shard_map/reduce_scatter | solution.py:23
Sparse Core Ops, SparseCore 0:
  9.5 75.5 all-gather.1
  119.7 87.1 reduce-scatter.1

commit v2 on v1

v2 whole, which is shorter than its diff:
```python
import functools

import jax
import jax.numpy as jnp
from jax import lax
from jax.experimental import pallas as pl
from jax.experimental.pallas import tpu as pltpu
from jax.sharding import PartitionSpec as P

denominator = 1024.0
SIDE = 2
LANES = 256
VMEM = 60 * 2**20


def expert_weights(expert_ids, gate_nums, experts):
    gates = gate_nums.astype(jnp.float32) / denominator
    labels = jnp.arange(experts, dtype=jnp.int32)
    onehot = expert_ids[:, :, None] == labels[None, None, :]
    return jnp.sum(jnp.where(onehot, gates[:, :, None], 0.0), axis=1)


def kernel(
    n, local,
    tokens, weights, w_gate, w_up, w_down, out,
    rows, factors, gate, up, down, hidden, part, from_side, from_line,
    load_sem, weight_send, weight_recv, line_send, line_recv, side_send, side_recv,
    back_side_send, back_side_recv, back_line_send, back_line_recv,
):
    depth = n // SIDE
    me = lax.axis_index("ep")
    z, y = me // SIDE, me % SIDE
    partner = z * SIDE + (SIDE - 1 - y)
    other = SIDE - 1 - y
    ff = w_gate.shape[2]
    count = tokens.shape[0]
    width = tokens.shape[1]

    def remote(source, target, send, recv, device):
        return pltpu.make_async_remote_copy(
            src_ref=source, dst_ref=target, send_sem=send, recv_sem=recv,
            device_id={"ep": device}, device_id_type=pl.DeviceIdType.MESH,
        )

    own = pltpu.make_async_copy(tokens, rows.at[z, y], load_sem.at[0])
    own.start()
    loads = []
    for e in range(local):
        cut = pl.ds(e * ff, ff)
        loads.append(pltpu.make_async_copy(w_gate.at[e], gate.at[e], load_sem.at[1 + 3 * e]))
        loads.append(pltpu.make_async_copy(w_up.at[e], up.at[e], load_sem.at[2 + 3 * e]))
        loads.append(pltpu.make_async_copy(w_down.at[e], down.at[cut], load_sem.at[3 + 3 * e]))
    for load in loads:
        load.start()

    barrier = pltpu.get_barrier_semaphore()
    for k in range(1, n):
        pl.semaphore_signal(
            barrier, inc=1, device_id={"ep": (me + k) % n}, device_id_type=pl.DeviceIdType.MESH
        )
    pl.semaphore_wait(barrier, n - 1)

    own.wait()

    def side_copy(o):
        return remote(rows.at[o, y], rows.at[o, y], side_send.at[o], side_recv.at[o], partner)

    def line_copy(k):
        there = ((z + k) % depth) * SIDE + y
        return remote(rows.at[z, y], rows.at[z, y], line_send.at[k], line_recv.at[z], there)

    def weight_copy(k):
        there = (me + k) % n
        return remote(weights.at[there], factors.at[me], weight_send.at[k], weight_recv.at[me], there)

    def part_copy(o):
        return remote(
            part.at[o, other], from_side.at[o], back_side_send.at[o], back_side_recv.at[o], partner
        )

    def sum_copy(o):
        there = o * SIDE + y
        return remote(
            part.at[o, y], from_line.at[z], back_line_send.at[o], back_line_recv.at[z], there
        )

    side_copy(z).start()
    for k in range(1, n):
        weight_copy(k).start()
    for k in range(1, depth):
        line_copy(k).start()
    factors[me] = weights[me]
    for load in loads:
        load.wait()
    for k in range(1, n):
        source = (me + k) % n
        remote(
            factors.at[source], factors.at[source], weight_send.at[k], weight_recv.at[source], partner
        ).wait_recv()

    turn = 1 - 2 * (z // (depth // 2))

    def origin(s):
        return (z + turn * s + depth) % depth

    def gather_next(o):
        remote(
            rows.at[o, y], rows.at[o, y], line_send.at[0], line_recv.at[o], partner
        ).wait_recv()
        side_copy(o).start()

    def finish(o):
        remote(
            from_side.at[o], from_side.at[o], back_side_send.at[o], back_side_recv.at[o], partner
        ).wait_recv()

    def pass_back(o):
        finish(o)
        total = part[o, y].astype(jnp.float32) + from_side[o].astype(jnp.float32)
        part[o, y] = total.astype(jnp.bfloat16)
        sum_copy(o).start()

    def step(s, carry):
        o = origin(s)
        remote(
            rows.at[o, other], rows.at[o, other], side_send.at[o], side_recv.at[o], partner
        ).wait_recv()
        scale = jnp.concatenate([factors[o * SIDE + i].T for i in range(SIDE)], axis=0)
        for e in range(local):
            column = scale[:, e : e + 1]

            def tile(t, carry):
                cut = pl.ds(pl.multiple_of(t * LANES, LANES), LANES)
                block = rows[o].reshape(SIDE * count, width)
                g = jnp.dot(block, gate[e, :, cut], preferred_element_type=jnp.float32)
                u = jnp.dot(block, up[e, :, cut], preferred_element_type=jnp.float32)
                h = g / (1.0 + jnp.exp(-g)) * u * column
                place = pl.ds(pl.multiple_of(e * ff + t * LANES, LANES), LANES)
                hidden[:, place] = h.astype(jnp.bfloat16)
                return carry

            lax.fori_loop(0, ff // LANES, tile, 0)

        @pl.when(s + 1 < depth)
        def _():
            gather_next(origin(s + 1))

        def spread(t, carry):
            cut = pl.ds(pl.multiple_of(t * LANES, LANES), LANES)
            result = jnp.dot(hidden[...], down[:, cut], preferred_element_type=jnp.float32)
            part[o, :, :, cut] = result.astype(jnp.bfloat16).reshape(SIDE, count, LANES)
            return carry

        lax.fori_loop(0, width // LANES, spread, 0)
        part_copy(o).start()

        @pl.when(s >= 2)
        def _():
            pass_back(origin(s - 1))

        return carry

    lax.fori_loop(0, depth, step, 0)
    if depth > 1:
        pass_back(origin(depth - 1))
    finish(z)
    total = part[z, y].astype(jnp.float32) + from_side[z].astype(jnp.float32)
    for s in range(1, depth):
        o = origin(s)
        remote(
            from_line.at[o], from_line.at[o], back_line_send.at[o], back_line_recv.at[o], partner
        ).wait_recv()
        total = total + from_line[o].astype(jnp.float32)
    out[...] = total.astype(jnp.bfloat16)
    for k in range(1, n):
        weight_copy(k).wait_send()
    for k in range(1, depth):
        line_copy(k).wait_send()
    for o in range(depth):
        side_copy(o).wait_send()
        part_copy(o).wait_send()
    for k in range(1, depth):
        sum_copy((z + k) % depth).wait_send()


def fused(tokens, expert_ids, gate_nums, w_gate, w_up, w_down, n):
    count, width = tokens.shape
    local, _, ff = w_gate.shape
    depth = n // SIDE
    weight = expert_weights(expert_ids, gate_nums, local * n)
    pad = -local % 8
    weights = jnp.pad(weight.T.reshape(n, local, count), ((0, 0), (0, pad), (0, 0)))
    kind = tokens.dtype
    dma = pltpu.SemaphoreType.DMA
    vmem = pl.BlockSpec(memory_space=pltpu.VMEM)
    hbm = pl.BlockSpec(memory_space=pl.ANY)
    return pl.pallas_call(
        functools.partial(kernel, n, local),
        out_shape=jax.ShapeDtypeStruct((count, width), kind),
        in_specs=[hbm, vmem, hbm, hbm, hbm],
        out_specs=vmem,
        scratch_shapes=[
            pltpu.VMEM((depth, SIDE, count, width), kind),
            pltpu.VMEM((n, local + pad, count), jnp.float32),
            pltpu.VMEM((local, width, ff), kind),
            pltpu.VMEM((local, width, ff), kind),
            pltpu.VMEM((local * ff, width), kind),
            pltpu.VMEM((SIDE * count, local * ff), kind),
            pltpu.VMEM((depth, SIDE, count, width), kind),
            pltpu.VMEM((depth, count, width), kind),
            pltpu.VMEM((depth, count, width), kind),
            dma((1 + 3 * local,)),
            dma((n,)), dma((n,)),
            dma((depth,)), dma((depth,)),
            dma((depth,)), dma((depth,)),
            dma((depth,)), dma((depth,)),
            dma((depth,)), dma((depth,)),
        ],
        compiler_params=pltpu.CompilerParams(
            collective_id=0, has_side_effects=True, vmem_limit_bytes=VMEM
        ),
    )(tokens, weights, w_gate, w_up, w_down)


def plain(tokens, expert_ids, gate_nums, w_gate, w_up, w_down, n):
    weight = expert_weights(expert_ids, gate_nums, w_gate.shape[0] * n)
    weights = lax.all_to_all(weight, "ep", split_axis=1, concat_axis=0, tiled=True)
    rows = lax.all_gather(tokens, "ep", axis=0, tiled=True)
    gate = jnp.einsum("td,xdf->xtf", rows, w_gate, preferred_element_type=jnp.float32)
    up = jnp.einsum("td,xdf->xtf", rows, w_up, preferred_element_type=jnp.float32)
    hidden = (jax.nn.silu(gate) * up * weights.T[:, :, None]).astype(jnp.bfloat16)
    result = jnp.einsum("xtf,xfd->td", hidden, w_down, preferred_element_type=jnp.float32)
    return lax.psum_scatter(
        result.astype(jnp.bfloat16), "ep", scatter_dimension=0, tiled=True
    )


def shards(n, tokens, expert_ids, gate_nums, w_gate, w_up, w_down):
    count, width = tokens.shape
    local, _, ff = w_gate.shape
    held = 3 * n * count * width + 3 * local * width * ff + 2 * count * local * ff
    fits = 2 * held < VMEM - 4 * 2**20
    shaped = n % (2 * SIDE) == 0 and count % 128 == 0 and ff % LANES == 0 and width % LANES == 0
    plan = fused if fits and shaped else plain
    return plan(tokens, expert_ids, gate_nums, w_gate, w_up, w_down, n)


def solution(mesh):
    placed = (
        P(("dp", "ep"), None),
        P(("dp", "ep"), None),
        P(("dp", "ep"), None),
        P("ep", None, None),
        P("ep", None, None),
        P("ep", None, None),
    )
    return jax.shard_map(
        functools.partial(shards, mesh.shape["ep"]),
        mesh=mesh, in_specs=placed, out_specs=P(("dp", "ep"), None), check_vma=False,
    )
```

time: 214 us -> 150 us (0.70)
  waiting for transfers between devices: 156 us -> 0 us
  Pallas kernels: 0 us -> 146 us
  matrix products: 34.5 us -> 0 us
  between operations: 13.4 us -> 0.01 us
  starting transfers between devices: 7.35 us -> 0 us
  local copies, waits for them, and re-layouts: 0 us -> 2.5 us
    pallas_call x0 -> x1, Pallas kernels: none -> 146 us  [fused(): pl.pallas_call(functools.partial(kernel, n, local), out_shape=jax.ShapeDt...]
    reduce_scatter x1 -> x0, waiting for transfers between devices: 87.4 us -> none  [shards(): lax.psum_scatter(result.astype(jnp.bfloat16), 'ep', scatter_dimension=0,...]
    all_gather x1 -> x0, waiting for transfers between devices: 68.4 us -> none  [shards(): rows = lax.all_gather(tokens, 'ep', axis=0, tiled=True)]
    dot_general x2 -> x0, matrix products: 34.5 us -> none  [the longest x1 22.8 us: shards(): jnp.einsum('xtf,xfd->td', hidden, w_down, preferred_element_type=jnp.floa...]
    all_to_all x1 -> x0, starting transfers between devices: 7.31 us -> none  [shards(): lax.all_to_all(weight, 'ep', split_axis=1, concat_axis=0, tiled=True)]
  transfers between devices with their start and end apart: 3 -> 0, of which waited for: 2 -> 0; matrix products, arithmetic and copies ran while one was open for 6% -> 0% of each run, Pallas kernels for 0% -> 0%
where the time goes in v2:
time: 150 us
  Pallas kernels  146 us (97%)
  local copies, waits for them, and re-layouts  2.5 us (2%)
    pallas_call x1, Pallas kernels, fused(): pl.pallas_call(functools.partial(kernel, n, local), out_shape=jax.ShapeDt...  146 us

profile of v2, /device:TPU:0, one launch (start us, length us, event | category | flops | bytes accessed | tf_op | source)
XLA Modules:
  0.0 150.2 jit_solution(5803470050026291737)
XLA Ops:
  0.0 0.7 convert_multiply_fusion
  0.7 0.7 select_reduce_fusion
  1.4 0.6 pad.4.weights
  2.0 146.3 %shard_map.64 = bf16[128,2048]{1,0:T(8,128)(2,1)} custom-call(bf16[128,2048]{1,0:T(8,128)(2,1)} %tokens.1, f32[8,8,128]{2,1,0:T(8,128)} %pad.4.weights, bf16[2,2048,768]{2,1,0:T(8,128)(2,1)} %w_gate.1, bf16[2,2048,768]{2,1,0:T(8,128)(2,1)} %w_up.1, bf16[2,768,2048]{2,1,0:T(8,128)(2,1)} %w_down.1), custom_call_target="tpu_custom_call" | custom-call | tf_op jit(solution)/shard_map/pallas_call | solution.py:197
  148.3 1.9 %copy.10 = bf16[128,2048]{1,0:T(8,128)(2,1)} copy(bf16[128,2048]{1,0:T(8,128)(2,1)} %shard_map.64) | data formatting | bytes 1048576

commit v3 on v2

--- a/solution.py
+++ b/solution.py
@@ -21,7 +21,7 @@
 
 
 def kernel(
-    n, local,
+    n, local, messages,
     tokens, weights, w_gate, w_up, w_down, out,
     rows, factors, gate, up, down, hidden, part, from_side, from_line,
     load_sem, weight_send, weight_recv, line_send, line_recv, side_send, side_recv,
@@ -30,11 +30,15 @@
     depth = n // SIDE
     me = lax.axis_index("ep")
     z, y = me // SIDE, me % SIDE
-    partner = z * SIDE + (SIDE - 1 - y)
     other = SIDE - 1 - y
+    partner = z * SIDE + other
     ff = w_gate.shape[2]
     count = tokens.shape[0]
     width = tokens.shape[1]
+    last = depth - 1
+    late = [m for m, (_, _, first) in enumerate(messages) if not first]
+    early = [m for m, (_, _, first) in enumerate(messages) if first]
+    cuts = [pl.ds(start, size) for start, size, _ in messages]
 
     def remote(source, target, send, recv, device):
         return pltpu.make_async_remote_copy(
@@ -59,37 +63,111 @@
             barrier, inc=1, device_id={"ep": (me + k) % n}, device_id_type=pl.DeviceIdType.MESH
         )
     pl.semaphore_wait(barrier, n - 1)
-
     own.wait()
 
-    def side_copy(o):
-        return remote(rows.at[o, y], rows.at[o, y], side_send.at[o], side_recv.at[o], partner)
-
-    def line_copy(k):
-        there = ((z + k) % depth) * SIDE + y
-        return remote(rows.at[z, y], rows.at[z, y], line_send.at[k], line_recv.at[z], there)
+    def side_copy(o, row, m):
+        ref = rows.at[o, row, cuts[m]]
+        return remote(ref, ref, side_send.at[o, m], side_recv.at[o, m], partner)
+
+    def line_copy(o, row, m, way):
+        ref = rows.at[o, row, cuts[m]]
+        there = me + SIDE * (1 - 2 * way)
+        return remote(
+            ref, ref, line_send.at[way, o, row, m], line_recv.at[o, row, m], there
+        )
+
+    def onward(o, row, m, act):
+        @pl.when((o <= z) & (z < last))
+        def _():
+            act(line_copy(o, row, m, 0))
+
+        @pl.when((o >= z) & (z > 0))
+        def _():
+            act(line_copy(o, row, m, 1))
+
+    def start(copy):
+        copy.start()
+
+    def wait_send(copy):
+        copy.wait_send()
 
     def weight_copy(k):
         there = (me + k) % n
         return remote(weights.at[there], factors.at[me], weight_send.at[k], weight_recv.at[me], there)
 
-    def part_copy(o):
+    def back_side(o, m):
         return remote(
-            part.at[o, other], from_side.at[o], back_side_send.at[o], back_side_recv.at[o], partner
-        )
-
-    def sum_copy(o):
-        there = o * SIDE + y
+            part.at[o, other, cuts[m]], from_side.at[o, cuts[m]],
+            back_side_send.at[o, m], back_side_recv.at[o, m], partner,
+        )
+
+    def back_line(o, row, m, way):
+        there = me + SIDE * (1 - 2 * way)
         return remote(
-            part.at[o, y], from_line.at[z], back_line_send.at[o], back_line_recv.at[z], there
-        )
-
-    side_copy(z).start()
+            part.at[o, row, cuts[m]], from_line.at[way, o, row, cuts[m]],
+            back_line_send.at[o, row, m], back_line_recv.at[way, o, row, m], there,
+        )
+
+    def each_back(o, row, m, act):
+        @pl.when(o > z)
+        def _():
+            act(back_line(o, row, m, 0))
+
+        @pl.when(o < z)
+        def _():
+            act(back_line(o, row, m, 1))
+
+    for m in early:
+        side_copy(z, y, m).start()
     for k in range(1, n):
         weight_copy(k).start()
-    for k in range(1, depth):
-        line_copy(k).start()
+    for m in late:
+        onward(z, y, m, start)
+        side_copy(z, y, m).start()
+    for m in early:
+        onward(z, y, m, start)
     factors[me] = weights[me]
+
+    @pl.when(z == 0)
+    def _():
+        from_line[0] = jnp.zeros_like(from_line[0])
+
+    @pl.when(z == last)
+    def _():
+        from_line[1] = jnp.zeros_like(from_line[1])
+
+    for m in early:
+        side_copy(z, other, m).wait_recv()
+        onward(z, other, m, start)
+
+    turn = 1 - 2 * (z // (depth // 2))
+    pairs = jnp.minimum(z, last - z)
+    middle = jnp.minimum(pairs, 1)
+
+    def nearest(s):
+        both = z + turn * ((s + 1) // 2) * (2 * (s % 2) - 1)
+        single = z + turn * (s - pairs)
+        return jnp.where(s <= 2 * pairs, both, single)
+
+    def rotation(s):
+        return (z + turn * s + depth) % depth
+
+    def gather(o):
+        for m in late:
+            line_copy(o, y, m, 0).wait_recv()
+            onward(o, y, m, start)
+            side_copy(o, y, m).start()
+        for m in early:
+            for row in range(SIDE):
+                line_copy(o, row, m, 0).wait_recv()
+                onward(o, row, m, start)
+
+    gather(nearest(1))
+
+    @pl.when(middle == 1)
+    def _():
+        gather(nearest(2))
+
     for load in loads:
         load.wait()
     for k in range(1, n):
@@ -98,33 +176,38 @@
             factors.at[source], factors.at[source], weight_send.at[k], weight_recv.at[source], partner
         ).wait_recv()
 
-    turn = 1 - 2 * (z // (depth // 2))
-
-    def origin(s):
-        return (z + turn * s + depth) % depth
-
-    def gather_next(o):
-        remote(
-            rows.at[o, y], rows.at[o, y], line_send.at[0], line_recv.at[o], partner
-        ).wait_recv()
-        side_copy(o).start()
-
-    def finish(o):
-        remote(
-            from_side.at[o], from_side.at[o], back_side_send.at[o], back_side_recv.at[o], partner
-        ).wait_recv()
+    def arrive(o, row, m):
+        @pl.when((o >= z) & (z > 0))
+        def _():
+            back_line(o, row, m, 0).wait_recv()
+
+        @pl.when((o <= z) & (z < last))
+        def _():
+            back_line(o, row, m, 1).wait_recv()
+
+    def wide(ref):
+        return ref[...].astype(jnp.float32)
 
     def pass_back(o):
-        finish(o)
-        total = part[o, y].astype(jnp.float32) + from_side[o].astype(jnp.float32)
-        part[o, y] = total.astype(jnp.bfloat16)
-        sum_copy(o).start()
+        way = (last + z - o) // depth
+        for m in early:
+            for row in range(SIDE):
+                arrive(o, row, m)
+                total = wide(part.at[o, row, cuts[m]]) + wide(from_line.at[way, o, row, cuts[m]])
+                part[o, row, cuts[m]] = total.astype(part.dtype)
+                each_back(o, row, m, start)
+        for m in late:
+            back_side(o, m).wait_recv()
+            arrive(o, y, m)
+            total = wide(part.at[o, y, cuts[m]]) + wide(from_line.at[way, o, y, cuts[m]])
+            total = total + wide(from_side.at[o, cuts[m]])
+            part[o, y, cuts[m]] = total.astype(part.dtype)
+            each_back(o, y, m, start)
 
     def step(s, carry):
-        o = origin(s)
-        remote(
-            rows.at[o, other], rows.at[o, other], side_send.at[o], side_recv.at[o], partner
-        ).wait_recv()
+        o = nearest(s)
+        for m in late:
+            side_copy(o, other, m).wait_recv()
         scale = jnp.concatenate([factors[o * SIDE + i].T for i in range(SIDE)], axis=0)
         for e in range(local):
             column = scale[:, e : e + 1]
@@ -141,10 +224,6 @@
 
             lax.fori_loop(0, ff // LANES, tile, 0)
 
-        @pl.when(s + 1 < depth)
-        def _():
-            gather_next(origin(s + 1))
-
         def spread(t, carry):
             cut = pl.ds(pl.multiple_of(t * LANES, LANES), LANES)
             result = jnp.dot(hidden[...], down[:, cut], preferred_element_type=jnp.float32)
@@ -152,35 +231,64 @@
             return carry
 
         lax.fori_loop(0, width // LANES, spread, 0)
-        part_copy(o).start()
-
-        @pl.when(s >= 2)
-        def _():
-            pass_back(origin(s - 1))
+
+        @pl.when(s + 2 + middle < depth)
+        def _():
+            gather(nearest(s + 2 + middle))
+
+        @pl.when(s > 0)
+        def _():
+            for m in late:
+                back_side(o, m).start()
+
+        @pl.when((s >= 2) & (middle == 0))
+        def _():
+            pass_back(rotation(s - 1))
 
         return carry
 
     lax.fori_loop(0, depth, step, 0)
-    if depth > 1:
-        pass_back(origin(depth - 1))
-    finish(z)
-    total = part[z, y].astype(jnp.float32) + from_side[z].astype(jnp.float32)
-    for s in range(1, depth):
-        o = origin(s)
-        remote(
-            from_line.at[o], from_line.at[o], back_line_send.at[o], back_line_recv.at[o], partner
-        ).wait_recv()
-        total = total + from_line[o].astype(jnp.float32)
-    out[...] = total.astype(jnp.bfloat16)
+    for m in late:
+        back_side(z, m).start()
+
+    def rest(s, carry):
+        pass_back(rotation(s))
+        return carry
+
+    lax.fori_loop(1 + (1 - middle) * (depth - 2), depth, rest, 0)
+
+    def collected(row, m):
+        arrive(z, row, m)
+        total = wide(part.at[z, row, cuts[m]])
+        return total + wide(from_line.at[0, z, row, cuts[m]]) + wide(from_line.at[1, z, row, cuts[m]])
+
+    for m in early:
+        part[z, other, cuts[m]] = collected(other, m).astype(part.dtype)
+        back_side(z, m).start()
+    for m in late + early:
+        total = collected(y, m)
+        back_side(z, m).wait_recv()
+        out[cuts[m]] = (total + wide(from_side.at[z, cuts[m]])).astype(out.dtype)
+
     for k in range(1, n):
         weight_copy(k).wait_send()
-    for k in range(1, depth):
-        line_copy(k).wait_send()
-    for o in range(depth):
-        side_copy(o).wait_send()
-        part_copy(o).wait_send()
-    for k in range(1, depth):
-        sum_copy((z + k) % depth).wait_send()
+    for m in early:
+        side_copy(z, y, m).wait_send()
+        back_side(z, m).wait_send()
+
+    def settle(o, carry):
+        for m in late:
+            side_copy(o, y, m).wait_send()
+            back_side(o, m).wait_send()
+            onward(o, y, m, wait_send)
+            each_back(o, y, m, wait_send)
+        for m in early:
+            for row in range(SIDE):
+                onward(o, row, m, wait_send)
+                each_back(o, row, m, wait_send)
+        return carry
+
+    lax.fori_loop(0, depth, settle, 0)
 
 
 def fused(tokens, expert_ids, gate_nums, w_gate, w_up, w_down, n):
@@ -190,12 +298,15 @@
     weight = expert_weights(expert_ids, gate_nums, local * n)
     pad = -local % 8
     weights = jnp.pad(weight.T.reshape(n, local, count), ((0, 0), (0, pad), (0, 0)))
+    unit = count // 8
+    messages = [(0, 3 * unit, False), (3 * unit, 3 * unit, False), (6 * unit, 2 * unit, True)]
+    size = len(messages)
     kind = tokens.dtype
     dma = pltpu.SemaphoreType.DMA
     vmem = pl.BlockSpec(memory_space=pltpu.VMEM)
     hbm = pl.BlockSpec(memory_space=pl.ANY)
     return pl.pallas_call(
-        functools.partial(kernel, n, local),
+        functools.partial(kernel, n, local, messages),
         out_shape=jax.ShapeDtypeStruct((count, width), kind),
         in_specs=[hbm, vmem, hbm, hbm, hbm],
         out_specs=vmem,
@@ -208,13 +319,13 @@
             pltpu.VMEM((SIDE * count, local * ff), kind),
             pltpu.VMEM((depth, SIDE, count, width), kind),
             pltpu.VMEM((depth, count, width), kind),
-            pltpu.VMEM((depth, count, width), kind),
+            pltpu.VMEM((2, depth, SIDE, count, width), kind),
             dma((1 + 3 * local,)),
             dma((n,)), dma((n,)),
-            dma((depth,)), dma((depth,)),
-            dma((depth,)), dma((depth,)),
-            dma((depth,)), dma((depth,)),
-            dma((depth,)), dma((depth,)),
+            dma((2, depth, SIDE, size)), dma((depth, SIDE, size)),
+            dma((depth, size)), dma((depth, size)),
+            dma((depth, size)), dma((depth, size)),
+            dma((depth, SIDE, size)), dma((2, depth, SIDE, size)),
         ],
         compiler_params=pltpu.CompilerParams(
             collective_id=0, has_side_effects=True, vmem_limit_bytes=VMEM
@@ -238,7 +349,7 @@
 def shards(n, tokens, expert_ids, gate_nums, w_gate, w_up, w_down):
     count, width = tokens.shape
     local, _, ff = w_gate.shape
-    held = 3 * n * count * width + 3 * local * width * ff + 2 * count * local * ff
+    held = 5 * n * count * width + 3 * local * width * ff + 2 * count * local * ff
     fits = 2 * held < VMEM - 4 * 2**20
     shaped = n % (2 * SIDE) == 0 and count % 128 == 0 and ff % LANES == 0 and width % LANES == 0
     plan = fused if fits and shaped else plain

time: 150 us -> 123 us (0.82)
  Pallas kernels: 146 us -> 119 us
    pallas_call x1, Pallas kernels: 146 us -> 119 us  [fused(): pl.pallas_call(functools.partial(kernel, n, local, messages), out_shape=j...]
where the time goes in v3:
time: 123 us
  Pallas kernels  119 us (97%)
  local copies, waits for them, and re-layouts  2.5 us (2%)
  other arithmetic  1.39 us (1%)
    pallas_call x1, Pallas kernels, fused(): pl.pallas_call(functools.partial(kernel, n, local, messages), out_shape=j...  119 us

profile of v3, /device:TPU:0, one launch (start us, length us, event | category | flops | bytes accessed | tf_op | source)
XLA Modules:
  0.0 123.0 jit_solution(8645281839493296989)
XLA Ops:
  0.0 0.7 convert_multiply_fusion
  0.7 0.7 select_reduce_fusion
  1.4 0.6 pad.4.weights
  2.0 119.1 %shard_map.64 = bf16[128,2048]{1,0:T(8,128)(2,1)} custom-call(bf16[128,2048]{1,0:T(8,128)(2,1)} %tokens.1, f32[8,8,128]{2,1,0:T(8,128)} %pad.4.weights, bf16[2,2048,768]{2,1,0:T(8,128)(2,1)} %w_gate.1, bf16[2,2048,768]{2,1,0:T(8,128)(2,1)} %w_up.1, bf16[2,768,2048]{2,1,0:T(8,128)(2,1)} %w_down.1), custom_call_target="tpu_custom_call" | custom-call | tf_op jit(solution)/shard_map/pallas_call | solution.py:308
  121.1 1.9 %copy.10 = bf16[128,2048]{1,0:T(8,128)(2,1)} copy(bf16[128,2048]{1,0:T(8,128)(2,1)} %shard_map.64) | data formatting | bytes 1048576

commit v4 on v3

--- a/solution.py
+++ b/solution.py
@@ -36,9 +36,11 @@
     count = tokens.shape[0]
     width = tokens.shape[1]
     last = depth - 1
-    late = [m for m, (_, _, first) in enumerate(messages) if not first]
-    early = [m for m, (_, _, first) in enumerate(messages) if first]
-    cuts = [pl.ds(start, size) for start, size, _ in messages]
+    late = [m for m, (_, _, side, _) in enumerate(messages) if not side]
+    early = [m for m, (_, _, side, _) in enumerate(messages) if side]
+    late_back = [m for m, (_, _, _, side) in enumerate(messages) if not side]
+    early_back = [m for m, (_, _, _, side) in enumerate(messages) if side]
+    cuts = [pl.ds(start, size) for start, size, _, _ in messages]
 
     def remote(source, target, send, recv, device):
         return pltpu.make_async_remote_copy(
@@ -190,13 +192,13 @@
 
     def pass_back(o):
         way = (last + z - o) // depth
-        for m in early:
+        for m in early_back:
             for row in range(SIDE):
                 arrive(o, row, m)
                 total = wide(part.at[o, row, cuts[m]]) + wide(from_line.at[way, o, row, cuts[m]])
                 part[o, row, cuts[m]] = total.astype(part.dtype)
                 each_back(o, row, m, start)
-        for m in late:
+        for m in late_back:
             back_side(o, m).wait_recv()
             arrive(o, y, m)
             total = wide(part.at[o, y, cuts[m]]) + wide(from_line.at[way, o, y, cuts[m]])
@@ -232,15 +234,15 @@
 
         lax.fori_loop(0, width // LANES, spread, 0)
 
+        @pl.when(s > 0)
+        def _():
+            for m in late_back:
+                back_side(o, m).start()
+
         @pl.when(s + 2 + middle < depth)
         def _():
             gather(nearest(s + 2 + middle))
 
-        @pl.when(s > 0)
-        def _():
-            for m in late:
-                back_side(o, m).start()
-
         @pl.when((s >= 2) & (middle == 0))
         def _():
             pass_back(rotation(s - 1))
@@ -248,7 +250,7 @@
         return carry
 
     lax.fori_loop(0, depth, step, 0)
-    for m in late:
+    for m in late_back:
         back_side(z, m).start()
 
     def rest(s, carry):
@@ -262,10 +264,10 @@
         total = wide(part.at[z, row, cuts[m]])
         return total + wide(from_line.at[0, z, row, cuts[m]]) + wide(from_line.at[1, z, row, cuts[m]])
 
-    for m in early:
+    for m in early_back:
         part[z, other, cuts[m]] = collected(other, m).astype(part.dtype)
         back_side(z, m).start()
-    for m in late + early:
+    for m in late_back + early_back:
         total = collected(y, m)
         back_side(z, m).wait_recv()
         out[cuts[m]] = (total + wide(from_side.at[z, cuts[m]])).astype(out.dtype)
@@ -274,17 +276,20 @@
         weight_copy(k).wait_send()
     for m in early:
         side_copy(z, y, m).wait_send()
+    for m in early_back:
         back_side(z, m).wait_send()
 
     def settle(o, carry):
         for m in late:
             side_copy(o, y, m).wait_send()
+            onward(o, y, m, wait_send)
+        for m in late_back:
             back_side(o, m).wait_send()
-            onward(o, y, m, wait_send)
             each_back(o, y, m, wait_send)
-        for m in early:
-            for row in range(SIDE):
+        for row in range(SIDE):
+            for m in early:
                 onward(o, row, m, wait_send)
+            for m in early_back:
                 each_back(o, row, m, wait_send)
         return carry
 
@@ -299,7 +304,7 @@
     pad = -local % 8
     weights = jnp.pad(weight.T.reshape(n, local, count), ((0, 0), (0, pad), (0, 0)))
     unit = count // 8
-    messages = [(0, 3 * unit, False), (3 * unit, 3 * unit, False), (6 * unit, 2 * unit, True)]
+    messages = [(0 * unit, 2 * unit, False, False), (2 * unit, 2 * unit, False, False), (4 * unit, 3 * unit, False, False), (7 * unit, 1 * unit, True, False)]
     size = len(messages)
     kind = tokens.dtype
     dma = pltpu.SemaphoreType.DMA

time: 123 us -> 110 us (0.89)
  Pallas kernels: 119 us -> 106 us
    pallas_call x1, Pallas kernels: 119 us -> 106 us  [fused(): pl.pallas_call(functools.partial(kernel, n, local, messages), out_shape=j...]
where the time goes in v4:
time: 110 us
  Pallas kernels  106 us (96%)
  local copies, waits for them, and re-layouts  2.5 us (2%)
  other arithmetic  1.39 us (1%)
    pallas_call x1, Pallas kernels, fused(): pl.pallas_call(functools.partial(kernel, n, local, messages), out_shape=j...  106 us

profile of v4, /device:TPU:0, one launch (start us, length us, event | category | flops | bytes accessed | tf_op | source)
XLA Modules:
  0.0 109.9 jit_solution(10869150915535954690)
XLA Ops:
  0.0 0.7 convert_multiply_fusion
  0.7 0.7 select_reduce_fusion
  1.4 0.6 pad.4.weights
  2.0 106.0 %shard_map.64 = bf16[128,2048]{1,0:T(8,128)(2,1)} custom-call(bf16[128,2048]{1,0:T(8,128)(2,1)} %tokens.1, f32[8,8,128]{2,1,0:T(8,128)} %pad.4.weights, bf16[2,2048,768]{2,1,0:T(8,128)(2,1)} %w_gate.1, bf16[2,2048,768]{2,1,0:T(8,128)(2,1)} %w_up.1, bf16[2,768,2048]{2,1,0:T(8,128)(2,1)} %w_down.1), custom_call_target="tpu_custom_call" | custom-call | tf_op jit(solution)/shard_map/pallas_call | solution.py:313
  108.0 1.9 %copy.10 = bf16[128,2048]{1,0:T(8,128)(2,1)} copy(bf16[128,2048]{1,0:T(8,128)(2,1)} %shard_map.64) | data formatting | bytes 1048576

commit v5 on v4

--- a/solution.py
+++ b/solution.py
@@ -224,7 +224,7 @@
                 hidden[:, place] = h.astype(jnp.bfloat16)
                 return carry
 
-            lax.fori_loop(0, ff // LANES, tile, 0)
+            lax.fori_loop(0, ff // LANES, tile, 0, unroll=True)
 
         def spread(t, carry):
             cut = pl.ds(pl.multiple_of(t * LANES, LANES), LANES)
@@ -232,7 +232,7 @@
             part[o, :, :, cut] = result.astype(jnp.bfloat16).reshape(SIDE, count, LANES)
             return carry
 
-        lax.fori_loop(0, width // LANES, spread, 0)
+        lax.fori_loop(0, width // LANES, spread, 0, unroll=True)
 
         @pl.when(s > 0)
         def _():
@@ -304,7 +304,7 @@
     pad = -local % 8
     weights = jnp.pad(weight.T.reshape(n, local, count), ((0, 0), (0, pad), (0, 0)))
     unit = count // 8
-    messages = [(0 * unit, 2 * unit, False, False), (2 * unit, 2 * unit, False, False), (4 * unit, 3 * unit, False, False), (7 * unit, 1 * unit, True, False)]
+    messages = [(0 * unit, 2 * unit, False, False), (2 * unit, 2 * unit, False, False), (4 * unit, 2 * unit, False, False), (6 * unit, 1 * unit, False, False), (7 * unit, 1 * unit, True, False)]
     size = len(messages)
     kind = tokens.dtype
     dma = pltpu.SemaphoreType.DMA

time: 110 us -> 107 us (0.973)
  Pallas kernels: 106 us -> 102 us
    pallas_call x1, Pallas kernels: 106 us -> 102 us  [fused(): pl.pallas_call(functools.partial(kernel, n, local, messages), out_shape=j...]
where the time goes in v5:
time: 107 us; the launch traced here: 106 us
  Pallas kernels  102 us (95%)
  local copies, waits for them, and re-layouts  2.5 us (2%)
  other arithmetic  1.39 us (1%)
    pallas_call x1, Pallas kernels, fused(): pl.pallas_call(functools.partial(kernel, n, local, messages), out_shape=j...  102 us

profile of v5, /device:TPU:0, one launch (start us, length us, event | category | flops | bytes accessed | tf_op | source)
XLA Modules:
  0.0 106.4 jit_solution(2916803801547462965)
XLA Ops:
  0.0 0.7 convert_multiply_fusion
  0.7 0.7 select_reduce_fusion
  1.4 0.6 pad.4.weights
  2.0 102.5 %shard_map.64 = bf16[128,2048]{1,0:T(8,128)(2,1)} custom-call(bf16[128,2048]{1,0:T(8,128)(2,1)} %tokens.1, f32[8,8,128]{2,1,0:T(8,128)} %pad.4.weights, bf16[2,2048,768]{2,1,0:T(8,128)(2,1)} %w_gate.1, bf16[2,2048,768]{2,1,0:T(8,128)(2,1)} %w_up.1, bf16[2,768,2048]{2,1,0:T(8,128)(2,1)} %w_down.1), custom_call_target="tpu_custom_call" | custom-call | tf_op jit(solution)/shard_map/pallas_call | solution.py:313
  104.5 1.9 %copy.10 = bf16[128,2048]{1,0:T(8,128)(2,1)} copy(bf16[128,2048]{1,0:T(8,128)(2,1)} %shard_map.64) | data formatting | bytes 1048576
